TPU v7x, 512 devices: a whole 4x4x16 slice. The times are simulated.
512 devices in a mesh: dp: 32 (over y, z_hi, core), tensor: 16 (over z_lo, x).
Axes of the slice: x: 4, y: 4, z: 16 (z_hi: 4, z_lo: 4; z = z_hi * 4 + z_lo), core: 2. Of those that a mesh axis runs over, the one named last changes fastest.
Arguments:
- acts: bfloat16 [12288, 4096], P('dp', 'tensor'), may hold values from -6 to 6
- grad_out: bfloat16 [12288, 4096], P('dp', 'tensor'), may hold values from -60 to 60
- gate_pre: bfloat16 [12288, 14336], P('dp', 'tensor'), may hold values from -6 to 6
- up_pre: bfloat16 [12288, 14336], P('dp', 'tensor'), may hold values from -6 to 6
- down_weight: bfloat16 [14336, 4096], P('tensor', 'dp'), may hold values from -0.09375 to 0.09375
- proj_in: bfloat16 [4096, 64], P('tensor'), may hold values from -0.09375 to 0.09375
- proj_out: bfloat16 [14336, 64], P('tensor'), may hold values from -0.046875 to 0.046875
- lengths: int32 [96], P('dp'), may hold values from 64 to 128
- query_ids: int32 [16], replicated, may hold values from 0 to 95
Outputs:
- gram: float32 [4096, 4096], P('dp', 'tensor')
- scores: float32 [16, 96], P(None, 'dp')
Inputs may be any that keep to these rules, and one draw needn't show every extreme that they name: `query_ids`: queries may repeat.
All inputs are finite; a program needn't handle non-finite values.
Results may differ from a plain program's by a relative error of at most 0.004.
Values may be sent and summed in bfloat16 or wider, within the bound.
No kernel may reach another device: no remote copies, remote signals or barrier semaphores. Data moves between devices by JAX's collectives and lax.ppermute only.
A program may use at most 64 MiB of HBM per device.

v0:
```python
import jax
import jax.numpy as jnp
from jax import lax
from jax.sharding import Mesh
from jax.sharding import PartitionSpec as P

TENSOR = ("tensor_0", "tensor_1")


def in_order(parts, dim):
    shape = list(parts.shape[1:])
    shape[dim] *= parts.shape[0]
    return jnp.moveaxis(parts, 0, dim).reshape(shape)


def stacked_from(array, axes, order):
    parts = array
    for k in order:
        parts = lax.all_gather(parts, axes[k])
    done = order[::-1]
    back = [done.index(k) for k in range(len(axes))]
    parts = parts.transpose(*back, *range(len(axes), parts.ndim))
    return parts.reshape(-1, *array.shape)


def whole_of(array, axes, order, dim):
    return in_order(stacked_from(array, axes, order), dim)


def filled_up(lines, count):
    spare = -len(lines) % count
    return jnp.pad(lines, [(0, spare)] + [(0, 0)] * (lines.ndim - 1))


def from_everyone(array, axis):
    count = lax.axis_size(axis)
    return lax.all_to_all(
        jnp.broadcast_to(array[None], (count, *array.shape)), axis, 0, 0, tiled=True
    )


def gather_directly(array, axis, dim):
    return in_order(from_everyone(array, axis), dim)


def split_up(array, dim, count):
    shape = array.shape
    parts = array.reshape(*shape[:dim], count, shape[dim] // count, *shape[dim + 1 :])
    return jnp.moveaxis(parts, dim, 0)


def sum_at_owner(array, axis, dim):
    count = lax.axis_size(axis)
    parts = lax.all_to_all(split_up(array, dim, count), axis, 0, 0, tiled=True)
    return jnp.sum(parts, axis=0)


def sum_by_parts(array, axes):
    padded = filled_up(array, lax.axis_size(axes))
    whole = gather_directly(sum_at_owner(padded, axes, 0), axes, 0)
    return lax.slice_in_dim(whole, 0, len(array)).reshape(array.shape)


def together(arrays, axis):
    flat, at, gathered = (jnp.concatenate([a.reshape(-1) for a in arrays]), 0, [])
    subtotal = sum_by_parts(flat, axis)
    for a in arrays:
        gathered.append(subtotal[at : at + a.size].reshape(a.shape))
        at += a.size
    return tuple(gathered)


def silu_slope(value):
    sigma = jax.nn.sigmoid(value)
    return sigma + value * sigma * (1.0 - sigma)


def body(acts, grad_out, gate_pre, up_pre, down_weight, proj_in, proj_out, lengths, query_ids):
    highest = lax.Precision.HIGHEST
    tokens_here = acts.shape[0]
    examples_here = lengths.shape[0]
    seq_len = tokens_here // examples_here
    full_grad = whole_of(grad_out, TENSOR, (0, 1), 1)
    hidden_grad = lax.dot_general(
        full_grad,
        lax.all_gather(down_weight, "dp", axis=1, tiled=True),
        (((1,), (1,)), ((), ())),
        preferred_element_type=jnp.float32,
    )
    gate_value = gate_pre.astype(jnp.float32)
    gate_grad = (hidden_grad * up_pre.astype(jnp.float32) * silu_slope(gate_value)).astype(
        jnp.bfloat16
    )
    out_part = jnp.dot(gate_grad, proj_out, preferred_element_type=jnp.float32)
    in_part = jnp.dot(acts, proj_in, preferred_element_type=jnp.float32)
    out_factor, in_factor = together((out_part, in_part), TENSOR)
    positions = lax.broadcasted_iota(jnp.int32, (examples_here, seq_len), 1)
    live = (positions < lengths[:, None]).astype(jnp.float32)
    out_factor = out_factor.reshape(examples_here, seq_len, -1) * live[:, :, None]
    in_factor = in_factor.reshape(examples_here, seq_len, -1)
    features = jnp.einsum("esa,esb->eab", out_factor, in_factor, precision=highest).reshape(
        examples_here, -1
    )
    width = features.shape[1]
    first_example = lax.axis_index("dp") * examples_here
    example_ids = first_example + lax.broadcasted_iota(jnp.int32, (1, examples_here), 1)
    selector = (query_ids[:, None] == example_ids).astype(jnp.float32)
    query_part = jnp.dot(selector, features, precision=highest)
    local_square = jnp.sum(features * features)
    query_feat, total_square = together((query_part, local_square), "dp")
    examples_all = examples_here * lax.axis_size("dp")
    norm_mean = total_square / examples_all + 1e-06
    col_width = width // lax.axis_size(TENSOR)
    own_cols = lax.dynamic_slice_in_dim(features, lax.axis_index(TENSOR) * col_width, col_width, 1)
    row_block = lax.all_to_all(features, "dp", split_axis=1, concat_axis=0, tiled=True)
    block = lax.dot_general(
        row_block,
        gather_directly(own_cols, "dp", 0),
        (((0,), (0,)), ((), ())),
        precision=highest,
        preferred_element_type=jnp.float32,
    )
    gram = block * (width / examples_all) / norm_mean
    scores = jnp.dot(query_feat, features.T, precision=highest) / norm_mean
    return (gram, scores)


def solution(mesh):
    split = Mesh(mesh.devices.reshape(mesh.shape["dp"], 4, 4), ("dp", "tensor_0", "tensor_1"))
    in_specs = (
        P("dp", TENSOR),
        P("dp", TENSOR),
        P("dp", TENSOR),
        P("dp", TENSOR),
        P(TENSOR, "dp"),
        P(TENSOR, None),
        P(TENSOR, None),
        P("dp"),
        P(),
    )
    out_specs = (P("dp", TENSOR), P(None, "dp"))
    return jax.shard_map(body, mesh=split, in_specs=in_specs, out_specs=out_specs, check_vma=False)
```

profile of v0, /device:TPU:1, one launch (start us, length us, event | category | flops | bytes accessed | tf_op | source)
XLA Modules:
  0.0 366.1 jit_solution(10889218226166880357)
XLA Ops:
  7.2 20.1 %all-gather = bf16[1536,256]{1,0:T(8,128)(2,1)} all-gather(bf16[384,256]{1,0:T(8,128)(2,1)} %param.10), channel_id=2, replica_groups=mesh['dp'=32,'tensor_0'=4,'tensor_1'=4] {'tensor_0'}, dimensions={0}, use_global_device_ids=true | all-gather | bytes 983040 | tf_op jit(solution)/shard_map/all_gather | solution.py:19
  27.4 0.7 all-gather.5.cloned.1.call-update
  28.4 50.3 %all-gather.7.cloned.1.call-done = bf16[16,384,256]{2,1,0:T(8,128)(2,1)} async-done(((bf16[4,384,256]{2,1,0:T(8,128)(2,1)}), bf16[16,384,256]{2,1,0:T(8,128)(2,1)}) %all-gather.7.cloned.1.call-update) | async-done | bytes 3145744 | tf_op jit(solution)/shard_map/all_gather | solution.py:19
  78.7 2.1 copy.42
  80.8 2.8 copy.43
  83.6 132.9 %all-gather.5.cloned.1.call-done = bf16[896,4096]{1,0:T(8,128)(2,1)} async-done(((bf16[896,128]{1,0:T(8,128)(2,1)}), bf16[896,4096]{1,0:T(8,128)(2,1)}) %all-gather.5.cloned.1.call-update) | async-done | bytes 7340048 | tf_op jit(solution)/shard_map/all_gather | solution.py:86
  216.5 8.0 %fusion.7 = f32[384,64]{1,0:T(8,128)S(1)} fusion(bf16[896,64]{0,1:T(8,128)(2,1)} %param.15, bf16[384,896]{1,0:T(8,128)(2,1)} %param.11, bf16[384,896]{1,0:T(8,128)(2,1)} %param.12, bf16[384,4096]{0,1:T(8,128)(2,1)} %bitcast.35, bf16[896,4096]{1,0:T(8,128)(2,1)} %all-gather.5.cloned.1.call-done), kind=kOutput, calls=%fused_computation.11 | convolution fusion | flops 2866741248 | bytes 12075008 | tf_op jit(solution)/shard_map/dot_general | solution.py:94
  224.6 0.2 copy.46
  224.8 12.5 %all_to_all.51 = f32[16,1,3072]{2,1,0:T(1,128)S(1)} all-to-all(f32[16,1,3072]{2,1,0:T(1,128)S(1)} %copy.46), channel_id=1, replica_groups=mesh['dp'=32,'tensor_0'=4,'tensor_1'=4] {'tensor_0','tensor_1'}, dimensions={0} | all-to-all | bytes 393216 | tf_op jit(solution)/shard_map/all_to_all | solution.py:54
  237.4 0.8 broadcast_in_dim.6
  238.2 3.9 %all-to-all-start.1 = ((f32[16,1,3072]{2,1,0:T(1,128)}), f32[16,1,3072]{2,1,0:T(1,128)S(1)}, u32[]{:S(2)}, u32[]{:S(2)}) async-start(f32[16,1,3072]{2,1,0:T(1,128)} %broadcast_in_dim.6), calls=%async_computation.1 | async-start | bytes 393216 | tf_op jit(solution)/shard_map/all_to_all | solution.py:37
  242.2 8.2 %all-to-all-done.1 = f32[16,1,3072]{2,1,0:T(1,128)S(1)} async-done(((f32[16,1,3072]{2,1,0:T(1,128)}), f32[16,1,3072]{2,1,0:T(1,128)S(1)}, u32[]{:S(2)}, u32[]{:S(2)}) %all-to-all-start.1) | async-done | bytes 196640 | tf_op jit(solution)/shard_map/all_to_all | solution.py:37
  250.4 0.5 slice_reduce_fusion.1
  251.1 1.2 multiply_reduce_fusion
  252.4 0.3 convolution_bitcast_fusion
  252.8 0.7 select_maximum_fusion
  253.4 1.1 all_to_all.42
  254.5 11.2 %all-to-all-start.4 = ((f32[32,1,2049]{2,1,0:T(1,128)}), f32[32,1,2049]{2,1,0:T(1,128)S(1)}, u32[]{:S(2)}, u32[]{:S(2)}) async-start(f32[32,1,2049]{2,1,0:T(1,128)} %all_to_all.42), calls=%async_computation.4 | async-start | bytes 557056 | tf_op jit(solution)/shard_map/all_to_all | solution.py:54
  265.8 0.7 copy.49
  266.5 19.6 %all-to-all-done.4 = f32[32,1,2049]{2,1,0:T(1,128)S(1)} async-done(((f32[32,1,2049]{2,1,0:T(1,128)}), f32[32,1,2049]{2,1,0:T(1,128)S(1)}, u32[]{:S(2)}, u32[]{:S(2)}) %all-to-all-start.4) | async-done | bytes 262304 | tf_op jit(solution)/shard_map/all_to_all | solution.py:54
  286.1 7.2 %all-to-all-start.2 = ((f32[3,32,128]{2,0,1:T(4,128)}), f32[3,32,128]{2,0,1:T(4,128)S(1)}, u32[]{:S(2)}, u32[]{:S(2)}) async-start(f32[3,32,128]{2,0,1:T(4,128)} %copy.49), calls=%async_computation.2 | async-start | bytes 131072 | tf_op jit(solution)/shard_map/all_to_all | solution.py:115
  293.4 14.8 %all-to-all-done.2 = f32[3,32,128]{2,0,1:T(4,128)S(1)} async-done(((f32[3,32,128]{2,0,1:T(4,128)}), f32[3,32,128]{2,0,1:T(4,128)S(1)}, u32[]{:S(2)}, u32[]{:S(2)}) %all-to-all-start.2) | async-done | bytes 49184 | tf_op jit(solution)/shard_map/all_to_all | solution.py:115
  308.2 0.9 broadcast_in_dim.8
  309.1 3.8 %all-to-all-start.5 = ((f32[32,1,2049]{2,1,0:T(1,128)}), f32[32,1,2049]{2,1,0:T(1,128)S(1)}, u32[]{:S(2)}, u32[]{:S(2)}) async-start(f32[32,1,2049]{2,1,0:T(1,128)} %broadcast_in_dim.8), calls=%async_computation.5 | async-start | bytes 557056 | tf_op jit(solution)/shard_map/all_to_all | solution.py:37
  312.9 17.7 %all-to-all-done.5 = f32[32,1,2049]{2,1,0:T(1,128)S(1)} async-done(((f32[32,1,2049]{2,1,0:T(1,128)}), f32[32,1,2049]{2,1,0:T(1,128)S(1)}, u32[]{:S(2)}, u32[]{:S(2)}) %all-to-all-start.5) | async-done | bytes 262304 | tf_op jit(solution)/shard_map/all_to_all | solution.py:37
  330.6 0.7 broadcast_in_dim.7
  331.3 9.4 %all-to-all-start.3 = ((f32[32,3,256]{2,1,0:T(4,128)}), f32[32,3,256]{2,1,0:T(4,128)S(1)}, u32[]{:S(2)}, u32[]{:S(2)}) async-start(f32[32,3,256]{2,1,0:T(4,128)} %broadcast_in_dim.7), calls=%async_computation.3 | async-start | bytes 262144 | tf_op jit(solution)/shard_map/all_to_all | solution.py:37
  340.7 0.7 reduce.5
  341.5 0.5 slice.25
  342.8 1.0 convolution_divide_fusion
  343.8 14.5 %all-to-all-done.3 = f32[32,3,256]{2,1,0:T(4,128)S(1)} async-done(((f32[32,3,256]{2,1,0:T(4,128)}), f32[32,3,256]{2,1,0:T(4,128)S(1)}, u32[]{:S(2)}, u32[]{:S(2)}) %all-to-all-start.3) | async-done | bytes 98336 | tf_op jit(solution)/shard_map/all_to_all | solution.py:37
  358.3 1.0 fusion.9
  (28 shorter events, 1.6 us)
Async XLA Ops:
  7.2 20.9 %copy-start = (bf16[384,256]{1,0:T(8,128)(2,1)S(1)}, bf16[384,256]{1,0:T(8,128)(2,1)}, u32[]{:S(2)}) copy-start(bf16[384,256]{1,0:T(8,128)(2,1)} %param.9) | copy-start | bytes 589828
  7.2 20.9 %copy-start.1 = (bf16[256,64]{0,1:T(8,128)(2,1)S(1)}, bf16[256,64]{0,1:T(8,128)(2,1)}, u32[]{:S(2)}) copy-start(bf16[256,64]{0,1:T(8,128)(2,1)} %param.14) | copy-start | bytes 98308
  7.2 71.5 %all-gather.7.cloned.1.call-start = ((), (), s32[]{:S(2)}) async-start(), calls=%async_computation.7 | async-start | bytes 3932160 | tf_op jit(solution)/shard_map/all_gather | solution.py:19
  27.3 189.2 %all-gather.5.cloned.1.call-start = ((), (), s32[]{:S(2)}) async-start(), calls=%async_computation.6 | async-start | bytes 7569408 | tf_op jit(solution)/shard_map/all_gather | solution.py:86
  224.5 17.7 %copy-start.3 = (s32[3]{0:T(128)S(1)}, s32[3]{0:T(128)}, u32[]{:S(2)}) copy-start(s32[3]{0:T(128)} %param.16) | copy-start | bytes 40
  224.8 27.6 %copy-start.2 = (s32[16]{0:T(128)S(1)}, s32[16]{0:T(128)}, u32[]{:S(2)}) copy-start(s32[16]{0:T(128)} %param.17) | copy-start | bytes 196
  238.2 12.2 %all-to-all-start.1 = ((f32[16,1,3072]{2,1,0:T(1,128)}), f32[16,1,3072]{2,1,0:T(1,128)S(1)}, u32[]{:S(2)}, u32[]{:S(2)}) async-start(f32[16,1,3072]{2,1,0:T(1,128)} %broadcast_in_dim.6), calls=%async_computation.1 | async-start | bytes 393216 | tf_op jit(solution)/shard_map/all_to_all | solution.py:37
  254.5 31.5 %all-to-all-start.4 = ((f32[32,1,2049]{2,1,0:T(1,128)}), f32[32,1,2049]{2,1,0:T(1,128)S(1)}, u32[]{:S(2)}, u32[]{:S(2)}) async-start(f32[32,1,2049]{2,1,0:T(1,128)} %all_to_all.42), calls=%async_computation.4 | async-start | bytes 557056 | tf_op jit(solution)/shard_map/all_to_all | solution.py:54
  286.1 22.1 %all-to-all-start.2 = ((f32[3,32,128]{2,0,1:T(4,128)}), f32[3,32,128]{2,0,1:T(4,128)S(1)}, u32[]{:S(2)}, u32[]{:S(2)}) async-start(f32[3,32,128]{2,0,1:T(4,128)} %copy.49), calls=%async_computation.2 | async-start | bytes 131072 | tf_op jit(solution)/shard_map/all_to_all | solution.py:115
  309.1 21.5 %all-to-all-start.5 = ((f32[32,1,2049]{2,1,0:T(1,128)}), f32[32,1,2049]{2,1,0:T(1,128)S(1)}, u32[]{:S(2)}, u32[]{:S(2)}) async-start(f32[32,1,2049]{2,1,0:T(1,128)} %broadcast_in_dim.8), calls=%async_computation.5 | async-start | bytes 557056 | tf_op jit(solution)/shard_map/all_to_all | solution.py:37
  331.3 27.0 %all-to-all-start.3 = ((f32[32,3,256]{2,1,0:T(4,128)}), f32[32,3,256]{2,1,0:T(4,128)S(1)}, u32[]{:S(2)}, u32[]{:S(2)}) async-start(f32[32,3,256]{2,1,0:T(4,128)} %broadcast_in_dim.7), calls=%async_computation.3 | async-start | bytes 262144 | tf_op jit(solution)/shard_map/all_to_all | solution.py:37
Sparse Core Ops, SparseCore 0:
  27.4 51.1 all-gather.6
  81.7 134.7 all-gather.4
where the time goes:
time: 367 us; the launch traced here: 366 us
  waiting for transfers between devices  259 us (71%)
  starting transfers between devices  35.5 us (10%)
  blocking collectives  32.5 us (9%)
  between operations  14.9 us (4%)
  matrix products  11.6 us (3%)
  local copies, waits for them, and re-layouts  11.1 us (3%)
    all_gather x1, waiting for transfers between devices, body(): lax.all_gather(down_weight, 'dp', axis=1, tiled=True)  133 us
    all_gather x1, waiting for transfers between devices, stacked_from(): parts = lax.all_gather(parts, axes[k])  50.3 us
    all_to_all x3, waiting for transfers between devices, from_everyone(): lax.all_to_all(jnp.broadcast_to(array[None], (count, *array.shape)), axis...  40.4 us
    all_gather x1, blocking collectives, stacked_from(): parts = lax.all_gather(parts, axes[k])  20.1 us
    all_to_all x1, waiting for transfers between devices, sum_at_owner(): parts = lax.all_to_all(split_up(array, dim, count), axis, 0, 0, tiled=True)  19.6 us
    all_to_all x3, starting transfers between devices, from_everyone(): lax.all_to_all(jnp.broadcast_to(array[None], (count, *array.shape)), axis...  17.1 us
    all_to_all x1, waiting for transfers between devices, body(): lax.all_to_all(features, 'dp', split_axis=1, concat_axis=0, tiled=True)  14.8 us
    all_to_all x1, blocking collectives, sum_at_owner(): parts = lax.all_to_all(split_up(array, dim, count), axis, 0, 0, tiled=True)  12.5 us
  transfers between devices with their start and end apart: 7, of which 7 were waited for; matrix products, arithmetic and copies ran while one was open for 2% of the time, Pallas kernels for 0%

commit v1 on v0

--- a/solution.py
+++ b/solution.py
@@ -83,7 +83,9 @@
     full_grad = whole_of(grad_out, TENSOR, (0, 1), 1)
     hidden_grad = lax.dot_general(
         full_grad,
-        lax.all_gather(down_weight, "dp", axis=1, tiled=True),
+        jnp.concatenate(
+            lax.all_to_all(jnp.stack([down_weight] * lax.axis_size("dp")), "dp", 0, 0), axis=1
+        ),
         (((1,), (1,)), ((), ())),
         preferred_element_type=jnp.float32,
     )

time: 367 us -> 570 us (1.55)
  blocking collectives: 32.5 us -> 345 us
  waiting for transfers between devices: 259 us -> 121 us
  starting transfers between devices: 35.5 us -> 58.2 us
    all_gather x1, blocking collectives: 20.1 us -> 331 us  [stacked_from(): parts = lax.all_gather(parts, axes[k])]
    all_gather x1 -> x0, waiting for transfers between devices: 133 us -> none  [body(): lax.all_gather(down_weight, 'dp', axis=1, tiled=True)]
    all_to_all x0 -> x1, starting transfers between devices: none -> 19.5 us  [body(): lax.all_to_all(jnp.stack([down_weight] * lax.axis_size('dp')), 'dp', 0, 0)]
  transfers between devices with their start and end apart: 7 -> 7, of which waited for: 7 -> 6; matrix products, arithmetic and copies ran while one was open for 2% -> 1% of each run, Pallas kernels for 0% -> 0%
where the time goes in v1:
time: 570 us
  blocking collectives  345 us (61%)
  waiting for transfers between devices  121 us (21%)
  starting transfers between devices  58.2 us (10%)
  local copies, waits for them, and re-layouts  16.3 us (3%)
  between operations  14.9 us (3%)
  matrix products  11.8 us (2%)
    all_gather x1, blocking collectives, stacked_from(): parts = lax.all_gather(parts, axes[k])  331 us
    all_gather x1, waiting for transfers between devices, stacked_from(): parts = lax.all_gather(parts, axes[k])  46.4 us
    all_to_all x3, waiting for transfers between devices, from_everyone(): lax.all_to_all(jnp.broadcast_to(array[None], (count, *array.shape)), axis...  40.4 us
    all_to_all x1, waiting for transfers between devices, sum_at_owner(): parts = lax.all_to_all(split_up(array, dim, count), axis, 0, 0, tiled=True)  19.6 us
    all_to_all x1, starting transfers between devices, body(): lax.all_to_all(jnp.stack([down_weight] * lax.axis_size('dp')), 'dp', 0, 0)  19.5 us
    all_to_all x3, starting transfers between devices, from_everyone(): lax.all_to_all(jnp.broadcast_to(array[None], (count, *array.shape)), axis...  17.1 us
    all_to_all x1, waiting for transfers between devices, body(): lax.all_to_all(features, 'dp', split_axis=1, concat_axis=0, tiled=True)  14.9 us
    all_to_all x1, starting transfers between devices, sum_at_owner(): parts = lax.all_to_all(split_up(array, dim, count), axis, 0, 0, tiled=True)  14.9 us
  transfers between devices with their start and end apart: 7, of which 6 were waited for; matrix products, arithmetic and copies ran while one was open for 1% of the time, Pallas kernels for 0%

profile of v1, /device:TPU:1, one launch (start us, length us, event | category | flops | bytes accessed | tf_op | source)
XLA Modules:
  0.0 569.5 jit_solution(13671894004950990890)
XLA Ops:
  7.2 1.1 copy.48
  8.3 4.1 stack.2
  12.4 19.5 %all-to-all-start = ((bf16[32,896,128]{1,2,0:T(8,128)(2,1)}), bf16[32,896,128]{1,2,0:T(8,128)(2,1)}, u32[]{:S(2)}, u32[]{:S(2)}) async-start(bf16[32,896,128]{1,2,0:T(8,128)(2,1)} %stack.2), calls=%async_computation | async-start | bytes 14680064 | tf_op jit(solution)/shard_map/all_to_all | solution.py:87
  32.0 331.1 %all-gather = bf16[1536,256]{1,0:T(8,128)(2,1)} all-gather(bf16[384,256]{1,0:T(8,128)(2,1)S(1)} %copy-done.1), channel_id=2, replica_groups=mesh['dp'=32,'tensor_0'=4,'tensor_1'=4] {'tensor_0'}, dimensions={0}, use_global_device_ids=true | all-gather | bytes 983040 | tf_op jit(solution)/shard_map/all_gather | solution.py:19
  363.5 46.4 %all-gather.4.cloned.1.call-done = bf16[16,384,256]{2,1,0:T(8,128)(2,1)} async-done(((bf16[4,384,256]{2,1,0:T(8,128)(2,1)}), bf16[16,384,256]{2,1,0:T(8,128)(2,1)}) %all-gather.4.cloned.1.call-update) | async-done | bytes 3145744 | tf_op jit(solution)/shard_map/all_gather | solution.py:19
  409.9 2.1 copy.46
  412.0 2.8 copy.47
  414.8 8.2 %fusion.7 = f32[384,64]{1,0:T(8,128)S(1)} fusion(bf16[896,64]{0,1:T(8,128)(2,1)} %param.15, bf16[384,896]{1,0:T(8,128)(2,1)} %param.11, bf16[384,896]{1,0:T(8,128)(2,1)} %param.12, bf16[384,4096]{0,1:T(8,128)(2,1)} %bitcast.38, bf16[896,4096]{0,1:T(8,128)(2,1)} %bitcast.7), kind=kOutput, calls=%fused_computation.11 | convolution fusion | flops 2866741248 | bytes 12075008 | tf_op jit(solution)/shard_map/dot_general | solution.py:96
  423.4 14.1 %all_to_all.56 = f32[16,1,3072]{2,1,0:T(1,128)S(1)} all-to-all(f32[16,1,3072]{2,1,0:T(1,128)S(1)} %copy.51), channel_id=1, replica_groups=mesh['dp'=32,'tensor_0'=4,'tensor_1'=4] {'tensor_0','tensor_1'}, dimensions={0} | all-to-all | bytes 393216 | tf_op jit(solution)/shard_map/all_to_all | solution.py:54
  437.6 0.8 broadcast_in_dim.6
  438.4 4.1 all-to-all-start.2
  442.6 8.2 %all-to-all-done.2 = f32[16,1,3072]{2,1,0:T(1,128)S(1)} async-done(((f32[16,1,3072]{2,1,0:T(1,128)}), f32[16,1,3072]{2,1,0:T(1,128)S(1)}, u32[]{:S(2)}, u32[]{:S(2)}) %all-to-all-start.2) | async-done | bytes 196640 | tf_op jit(solution)/shard_map/all_to_all | solution.py:37
  450.8 0.5 slice_reduce_fusion.1
  451.5 1.2 multiply_reduce_fusion
  452.8 0.3 convolution_bitcast_fusion
  453.1 0.7 select_maximum_fusion
  453.8 1.1 all_to_all.46
  454.9 14.9 %all-to-all-start.5 = ((f32[32,1,2049]{2,1,0:T(1,128)}), f32[32,1,2049]{2,1,0:T(1,128)S(1)}, u32[]{:S(2)}, u32[]{:S(2)}) async-start(f32[32,1,2049]{2,1,0:T(1,128)} %all_to_all.46), calls=%async_computation.5 | async-start | bytes 557056 | tf_op jit(solution)/shard_map/all_to_all | solution.py:54
  469.9 0.7 copy.54
  470.5 19.6 %all-to-all-done.5 = f32[32,1,2049]{2,1,0:T(1,128)S(1)} async-done(((f32[32,1,2049]{2,1,0:T(1,128)}), f32[32,1,2049]{2,1,0:T(1,128)S(1)}, u32[]{:S(2)}, u32[]{:S(2)}) %all-to-all-start.5) | async-done | bytes 262304 | tf_op jit(solution)/shard_map/all_to_all | solution.py:54
  490.1 6.6 %all-to-all-start.3 = ((f32[3,32,128]{2,0,1:T(4,128)}), f32[3,32,128]{2,0,1:T(4,128)S(1)}, u32[]{:S(2)}, u32[]{:S(2)}) async-start(f32[3,32,128]{2,0,1:T(4,128)} %copy.54), calls=%async_computation.3 | async-start | bytes 131072 | tf_op jit(solution)/shard_map/all_to_all | solution.py:117
  496.9 14.9 %all-to-all-done.3 = f32[3,32,128]{2,0,1:T(4,128)S(1)} async-done(((f32[3,32,128]{2,0,1:T(4,128)}), f32[3,32,128]{2,0,1:T(4,128)S(1)}, u32[]{:S(2)}, u32[]{:S(2)}) %all-to-all-start.3) | async-done | bytes 49184 | tf_op jit(solution)/shard_map/all_to_all | solution.py:117
  511.8 0.9 broadcast_in_dim.8
  512.7 3.7 all-to-all-start.6
  516.4 17.8 %all-to-all-done.6 = f32[32,1,2049]{2,1,0:T(1,128)S(1)} async-done(((f32[32,1,2049]{2,1,0:T(1,128)}), f32[32,1,2049]{2,1,0:T(1,128)S(1)}, u32[]{:S(2)}, u32[]{:S(2)}) %all-to-all-start.6) | async-done | bytes 262304 | tf_op jit(solution)/shard_map/all_to_all | solution.py:37
  534.2 0.7 broadcast_in_dim.7
  534.8 9.3 %all-to-all-start.4 = ((f32[32,3,256]{2,1,0:T(4,128)}), f32[32,3,256]{2,1,0:T(4,128)S(1)}, u32[]{:S(2)}, u32[]{:S(2)}) async-start(f32[32,3,256]{2,1,0:T(4,128)} %broadcast_in_dim.7), calls=%async_computation.4 | async-start | bytes 262144 | tf_op jit(solution)/shard_map/all_to_all | solution.py:37
  544.2 0.7 reduce.5
  545.0 0.5 slice.25
  546.3 1.0 convolution_divide_fusion
  547.3 14.4 %all-to-all-done.4 = f32[32,3,256]{2,1,0:T(4,128)S(1)} async-done(((f32[32,3,256]{2,1,0:T(4,128)}), f32[32,3,256]{2,1,0:T(4,128)S(1)}, u32[]{:S(2)}, u32[]{:S(2)}) %all-to-all-start.4) | async-done | bytes 98336 | tf_op jit(solution)/shard_map/all_to_all | solution.py:37
  561.7 1.0 fusion.9
  (31 shorter events, 1.8 us)
Async XLA Ops:
  7.2 356.0 %copy-start = (bf16[384,256]{1,0:T(8,128)(2,1)S(1)}, bf16[384,256]{1,0:T(8,128)(2,1)}, u32[]{:S(2)}) copy-start(bf16[384,256]{1,0:T(8,128)(2,1)} %param.9) | copy-start | bytes 589828
  12.4 19.6 %copy-start.1 = (bf16[384,256]{1,0:T(8,128)(2,1)S(1)}, bf16[384,256]{1,0:T(8,128)(2,1)}, u32[]{:S(2)}) copy-start(bf16[384,256]{1,0:T(8,128)(2,1)} %param.10) | copy-start | bytes 589828
  12.4 402.4 %all-to-all-start = ((bf16[32,896,128]{1,2,0:T(8,128)(2,1)}), bf16[32,896,128]{1,2,0:T(8,128)(2,1)}, u32[]{:S(2)}, u32[]{:S(2)}) async-start(bf16[32,896,128]{1,2,0:T(8,128)(2,1)} %stack.2), calls=%async_computation | async-start | bytes 14680064 | tf_op jit(solution)/shard_map/all_to_all | solution.py:87
  31.9 331.2 %copy-start.2 = (bf16[256,64]{0,1:T(8,128)(2,1)S(1)}, bf16[256,64]{0,1:T(8,128)(2,1)}, u32[]{:S(2)}) copy-start(bf16[256,64]{0,1:T(8,128)(2,1)} %param.14) | copy-start | bytes 98308
  32.0 378.0 %all-gather.4.cloned.1.call-start = ((), (), s32[]{:S(2)}) async-start(), calls=%async_computation.7 | async-start | bytes 3932160 | tf_op jit(solution)/shard_map/all_gather | solution.py:19
  423.0 19.5 %copy-start.4 = (s32[3]{0:T(128)S(1)}, s32[3]{0:T(128)}, u32[]{:S(2)}) copy-start(s32[3]{0:T(128)} %param.16) | copy-start | bytes 40
  423.3 29.4 %copy-start.3 = (s32[16]{0:T(128)S(1)}, s32[16]{0:T(128)}, u32[]{:S(2)}) copy-start(s32[16]{0:T(128)} %param.17) | copy-start | bytes 196
  438.4 12.4 %all-to-all-start.2 = ((f32[16,1,3072]{2,1,0:T(1,128)}), f32[16,1,3072]{2,1,0:T(1,128)S(1)}, u32[]{:S(2)}, u32[]{:S(2)}) async-start(f32[16,1,3072]{2,1,0:T(1,128)} %broadcast_in_dim.6), calls=%async_computation.2 | async-start | bytes 393216 | tf_op jit(solution)/shard_map/all_to_all | solution.py:37
  454.9 35.2 %all-to-all-start.5 = ((f32[32,1,2049]{2,1,0:T(1,128)}), f32[32,1,2049]{2,1,0:T(1,128)S(1)}, u32[]{:S(2)}, u32[]{:S(2)}) async-start(f32[32,1,2049]{2,1,0:T(1,128)} %all_to_all.46), calls=%async_computation.5 | async-start | bytes 557056 | tf_op jit(solution)/shard_map/all_to_all | solution.py:54
  490.1 21.7 %all-to-all-start.3 = ((f32[3,32,128]{2,0,1:T(4,128)}), f32[3,32,128]{2,0,1:T(4,128)S(1)}, u32[]{:S(2)}, u32[]{:S(2)}) async-start(f32[3,32,128]{2,0,1:T(4,128)} %copy.54), calls=%async_computation.3 | async-start | bytes 131072 | tf_op jit(solution)/shard_map/all_to_all | solution.py:117
  512.7 21.5 %all-to-all-start.6 = ((f32[32,1,2049]{2,1,0:T(1,128)}), f32[32,1,2049]{2,1,0:T(1,128)S(1)}, u32[]{:S(2)}, u32[]{:S(2)}) async-start(f32[32,1,2049]{2,1,0:T(1,128)} %broadcast_in_dim.8), calls=%async_computation.6 | async-start | bytes 557056 | tf_op jit(solution)/shard_map/all_to_all | solution.py:37
  534.8 26.9 %all-to-all-start.4 = ((f32[32,3,256]{2,1,0:T(4,128)}), f32[32,3,256]{2,1,0:T(4,128)S(1)}, u32[]{:S(2)}, u32[]{:S(2)}) async-start(f32[32,3,256]{2,1,0:T(4,128)} %broadcast_in_dim.7), calls=%async_computation.4 | async-start | bytes 262144 | tf_op jit(solution)/shard_map/all_to_all | solution.py:37
Sparse Core Ops, SparseCore 0:
  363.3 46.6 all-gather.3
